TPU v7x, 512 devices: a whole 4x8x8 slice. The times are simulated.
512 devices in a mesh: blk: 32 (over x_lo, y, core), col: 16 (over x_hi, z).
Axes of the slice: x: 4 (x_hi: 2, x_lo: 2; x = x_hi * 2 + x_lo), y: 8, z: 8, core: 2. Of those that a mesh axis runs over, the one named last changes fastest.
Arguments:
- documents: bfloat16 [24576, 768], P('blk'), may hold values from -6 to 6
- landmarks: bfloat16 [65536, 768], P(('blk', 'col')), may hold values from -6 to 6
- eigen_vectors: bfloat16 [65536, 256], P(('blk', 'col')), may hold values from -6 to 6
- land_degree: float32 [65536], P(('blk', 'col')), may hold values from 0.5 to 8
- eigen_values: float32 [256], replicated, may hold values from 0.005 to 0.05
- tile_mask: int32 [192, 512], P('blk'), may hold values from 0 to 1, as said below
- labels: int32 [24576], P(('blk', 'col')), may hold values from 0 to 999
Outputs:
- embedding: float32 [24576, 256], P(('blk', 'col'))
- centroids: float32 [1000, 256], replicated
Inputs may be any that keep to these rules, and one draw needn't show every extreme that they name: `tile_mask`: 1 marks a live tile of 128 documents by 128 landmarks; every document block has at least one live tile.
All inputs are finite; a program needn't handle non-finite values.
Results may differ from a plain program's by a relative error of at most 0.0041.
Values may be sent and summed in bfloat16 or wider, within the bound.
A program may use at most 64 MiB of HBM per device.

v0:
```python
import jax
import jax.numpy as jnp
from jax import lax
from jax.sharding import PartitionSpec as P

C = 1000
BLOCK = 128


def side_by_side(arrays, axis, dim, along):
    ends, at = ([], 0)
    for a in arrays[:-1]:
        at += a.shape[along]
        ends.append(at)
    both = jnp.concatenate(arrays, axis=along)
    return tuple(jnp.split(lax.all_gather(both, axis, axis=dim, tiled=True), ends, axis=along))


def split_up(value, dim, peers):
    shape = value.shape
    parts = value.reshape(*shape[:dim], peers, shape[dim] // peers, *shape[dim + 1 :])
    return jnp.moveaxis(parts, dim, 0)


def sent_and_summed(value, axis, dim):
    peers = lax.axis_size(axis)
    parts = lax.all_to_all(split_up(value, dim, peers), axis, 0, 0, tiled=True)
    return jnp.sum(parts, axis=0)


def in_one_piece(arrays, axis, dim, along):
    columns = [a.reshape(*a.shape[:along], -1) for a in arrays]
    both = jnp.concatenate(columns, axis=along)
    whole, at, outs = (sent_and_summed(both, axis, dim), 0, [])
    for a, column in zip(arrays, columns):
        share = whole[..., at : at + column.shape[along]]
        outs.append(share.reshape(*share.shape[:along], *a.shape[along:]))
        at += column.shape[along]
    return tuple(outs)


def body(documents, landmarks, eigen_vectors, land_degree, eigen_values, tile_mask, labels):
    inverse_width = 4.0 / documents.shape[1]
    land_rows = landmarks.shape[0]
    doc_rows = documents.shape[0]
    col_index = lax.axis_index("col")
    col_count = lax.axis_size("col")
    scaled = (
        eigen_vectors.astype(jnp.float32) * lax.rsqrt(land_degree)[:, None] / eigen_values[None, :]
    ).astype(jnp.bfloat16)
    doc_square = jnp.sum(jnp.square(documents.astype(jnp.float32)), 1)
    initial = (
        jnp.zeros((doc_rows, scaled.shape[1]), jnp.float32),
        jnp.zeros((doc_rows,), jnp.float32),
    )
    land_piece, vector_piece = side_by_side((landmarks, scaled), "blk", 0, 1)
    piece_rows = land_piece.shape[0]
    offsets = jnp.arange(piece_rows, dtype=jnp.int32)
    whole_rows = (
        offsets // land_rows * (land_rows * col_count) + col_index * land_rows + offsets % land_rows
    )
    live_cols = jnp.take(tile_mask, whole_rows // BLOCK, axis=1)

    def compute(state):
        land_square = jnp.sum(jnp.square(land_piece.astype(jnp.float32)), 1)
        products = jnp.einsum(
            "df,lf->dl", documents, land_piece, preferred_element_type=jnp.float32
        )
        keep = jnp.repeat(live_cols, BLOCK, axis=0).astype(jnp.float32)
        weights = (
            jnp.exp(inverse_width * (2.0 * products - doc_square[:, None] - land_square[None, :]))
            * keep
        )
        total = jnp.dot(
            weights.astype(jnp.bfloat16), vector_piece, preferred_element_type=jnp.float32
        )
        return (total, jnp.sum(weights, 1))

    projection, degree = lax.cond(jnp.any(live_cols > 0), compute, lambda state: state, initial)
    projection, degree = in_one_piece((projection, degree), "col", 0, 1)
    embedding = projection * lax.rsqrt(degree)[:, None]
    unit_rows = embedding * lax.rsqrt(jnp.sum(jnp.square(embedding), 1, keepdims=True) + 1e-06)
    one_hot = (jnp.arange(C, dtype=jnp.int32)[:, None] == labels[None, :]).astype(jnp.float32)
    partial_sums = jnp.dot(
        one_hot, unit_rows, precision=lax.Precision.HIGHEST, preferred_element_type=jnp.float32
    )
    centroids = lax.psum(partial_sums, ("blk", "col"))
    return (embedding, centroids)


def solution(mesh):
    placed = (
        P("blk", None),
        P(("blk", "col"), None),
        P(("blk", "col"), None),
        P(("blk", "col")),
        P(),
        P("blk", None),
        P(("blk", "col")),
    )
    return jax.shard_map(
        body, mesh=mesh, in_specs=placed, out_specs=(P(("blk", "col"), None), P()), check_vma=False
    )
```

profile of v0, /device:TPU:23, one launch (start us, length us, event | category | flops | bytes accessed | tf_op | source)
XLA Modules:
  0.0 429.9 jit_solution(15334240320638322248)
XLA Ops:
  7.2 0.7 rsqrt.15
  8.0 0.9 divide_convert_fusion
  8.9 1.7 pad_maximum_fusion.1
  10.6 0.9 copy.11
  11.5 0.1 compare_select_fusion
  11.6 10.8 %gather_fusion = s32[4096,6]{1,0:T(8,128)S(1)} fusion(s32[6,512]{0,1:T(8,128)S(1)} %copy.11, s32[4096]{0:T(1024)S(1)} %broadcast_clamp_fusion), kind=kCustom, calls=%fused_computation | custom fusion | bytes 212992 | tf_op jit(solution)/shard_map/jit(_take)/gather | solution.py:62
  22.5 3.8 compare_reduce_fusion
  27.0 0.2 convert_element_type.29
  27.1 62.1 %all-gather.2.cloned.1.call-done = bf16[4096,1024]{1,0:T(8,128)(2,1)} async-done(((bf16[128,1024]{1,0:T(8,128)(2,1)}), bf16[4096,1024]{1,0:T(8,128)(2,1)}) %all-gather.2.cloned.1.call-update) | async-done | bytes 8388624 | tf_op jit(solution)/shard_map/all_gather | solution.py:16
  89.2 17.6 %conditional.1 = (f32[16,48,256]{2,1,0:T(8,128)S(1)}, f32[16,48,1]{2,1,0:T(8,128)S(1)}) conditional(s32[]{:T(128)} %convert_element_type.26, () %tuple.20, (bf16[4096,1024]{1,0:T(8,128)(2,1)}, bf16[768,768]{1,0:T(8,128)(2,1)S(1)}, f32[768,768]{1,0:T(8,128)S(1)}, s32[6,4096]{0,1:T(8,128)}) %tuple.37), branch_computations={%region_1.2_spmd, %region_2.6_spmd} | conditional | flops 6475106304 | bytes 65716268 | solution.py:79
  89.2 2.9 copy.12
  92.1 1.1 convert_element_type.19
  93.2 0.2 multiply_reduce_fusion.1
  93.4 4.4 %multiply_reduce_fusion = f32[4096]{0:T(1024)S(1)} fusion(bf16[4096,1024]{1,0:T(8,128)(2,1)} %get-tuple-element.17), kind=kLoop, calls=%fused_computation.2 | loop fusion | flops 9433088 | bytes 6307840 | tf_op jit(solution)/shard_map/cond/branch_1_fun/reduce_sum | solution.py:65
  97.8 6.9 %fusion = (f32[768]{0:T(1024)S(1)}, bf16[768,4096]{1,0:T(8,128)(2,1)S(1)}) fusion(f32[6,4096]{1,0:T(8,128)S(1)} %convert_element_type.19, f32[4096]{0:T(1024)S(1)} %multiply_reduce_fusion, f32[768]{0:T(1024)S(1)} %multiply_reduce_fusion.1, bf16[768,768]{1,0:T(8,128)(2,1)S(1)} %get-tuple-element.16, bf16[4096,1024]{1,0:T(8,128)(2,1)S(1)} %copy-done), kind=kOutput, calls=%fused_computation.3 | convolution fusion | flops 4853857280 | bytes 13917184 | tf_op jit(solution)/shard_map/cond/branch_1_fun/df,lf->dl/dot_general | solution.py:66
  104.7 1.8 fusion.4
  106.5 0.3 concatenate.17
  106.8 0.1 pad_maximum_fusion
  106.9 38.2 %all_to_all.5 = f32[16,48,257]{2,1,0:T(8,128)S(1)} all-to-all(f32[16,48,257]{2,1,0:T(8,128)S(1)} %pad_maximum_fusion), channel_id=1, replica_groups=mesh['blk'=32,'col'=16] {'col'}, dimensions={0} | all-to-all | bytes 1579008 | tf_op jit(solution)/shard_map/all_to_all | solution.py:27
  145.2 0.1 fusion.13
  145.3 0.2 multiply_reduce_fusion.2
  145.5 1.6 fusion.6
  147.1 273.7 %all-reduce.2.cloned.1.call-done = f32[1000,256]{1,0:T(8,128)} async-done(((f32[1000,256]{1,0:T(8,128)}), f32[1000,256]{1,0:T(8,128)}) %all-reduce.2.cloned.1.call-update) | async-done | bytes 1024016 | tf_op jit(solution)/shard_map/psum | solution.py:87
  420.8 2.2 copy.21
  (16 shorter events, 0.2 us)
Async XLA Ops:
  7.2 19.8 %copy-start.1 = (bf16[768,768]{1,0:T(8,128)(2,1)S(1)}, bf16[768,768]{1,0:T(8,128)(2,1)}, u32[]{:S(2)}) copy-start(bf16[768,768]{1,0:T(8,128)(2,1)} %param.9) | copy-start | bytes 3538948
  7.2 82.0 %all-gather.2.cloned.1.call-start = ((), (), s32[]{:S(2)}) async-start(), calls=%async_computation.1 | async-start | bytes 8650752 | tf_op jit(solution)/shard_map/all_gather | solution.py:16
  10.6 410.2 %all-reduce.2.cloned.1.call-start = ((), (), s32[]{:S(2)}) async-start(), calls=%async_computation.2 | async-start | bytes 2048000 | tf_op jit(solution)/shard_map/psum | solution.py:87
  89.2 56.3 %copy-start.3 = (s32[48]{0:T(128)S(1)}, s32[48]{0:T(128)}, u32[]{:S(2)}) copy-start(s32[48]{0:T(128)} %param.15) | copy-start | bytes 580
  92.1 5.7 %copy-start = (bf16[4096,1024]{1,0:T(8,128)(2,1)S(1)}, bf16[4096,1024]{1,0:T(8,128)(2,1)}, u32[]{:S(2)}) copy-start(bf16[4096,1024]{1,0:T(8,128)(2,1)} %get-tuple-element.17) | copy-start | bytes 25165828 | tf_op jit(solution)/shard_map/cond
  145.5 277.5 %copy-start.2 = (f32[48,256]{1,0:T(8,128)}, f32[48,256]{1,0:T(8,128)S(1)}, u32[]{:S(2)}) copy-start(f32[48,256]{1,0:T(8,128)S(1)} %get-tuple-element.45) | copy-start | bytes 147460
Sparse Core Ops, SparseCore 0:
  10.7 78.4 all-gather.1
  147.2 273.4 all-reduce.1
where the time goes:
time: 430 us
  waiting for transfers between devices  336 us (78%)
  blocking collectives  38.2 us (9%)
  local copies, waits for them, and re-layouts  17.9 us (4%)
  between operations  14.8 us (3%)
  other arithmetic  12.7 us (3%)
  matrix products  10.3 us (2%)
    psum x1, waiting for transfers between devices, body(): centroids = lax.psum(partial_sums, ('blk', 'col'))  274 us
    all_gather x1, waiting for transfers between devices, side_by_side(): lax.all_gather(both, axis, axis=dim, tiled=True)  62.1 us
    all_to_all x1, blocking collectives, sent_and_summed(): parts = lax.all_to_all(split_up(value, dim, peers), axis, 0, 0, tiled=True)  38.2 us
    gather x1, local copies, waits for them, and re-layouts, body(): live_cols = jnp.take(tile_mask, whole_rows // BLOCK, axis=1)  10.8 us
  transfers between devices with their start and end apart: 2, of which 2 were waited for; matrix products, arithmetic and copies ran while one was open for 4% of the time, Pallas kernels for 0%

commit v1 on v0

--- a/solution.py
+++ b/solution.py
@@ -84,7 +84,7 @@
     partial_sums = jnp.dot(
         one_hot, unit_rows, precision=lax.Precision.HIGHEST, preferred_element_type=jnp.float32
     )
-    centroids = lax.psum(partial_sums, ("blk", "col"))
+    centroids = lax.psum(lax.psum(partial_sums, "blk"), "col")
     return (embedding, centroids)
 
 

time: 430 us -> 552 us (1.28)
  the two profiles are of different devices: /device:TPU:23 before, /device:TPU:8 now
where the time goes in v1:
time: 552 us
  waiting for transfers between devices  454 us (82%)
  blocking collectives  42.5 us (8%)
  local copies, waits for them, and re-layouts  17.9 us (3%)
  between operations  14.5 us (3%)
  other arithmetic  12.7 us (2%)
  matrix products  10.3 us (2%)
    psum x2, waiting for transfers between devices, body(): centroids = lax.psum(lax.psum(partial_sums, 'blk'), 'col')  392 us
    all_gather x1, waiting for transfers between devices, side_by_side(): lax.all_gather(both, axis, axis=dim, tiled=True)  61.7 us
    all_to_all x1, blocking collectives, sent_and_summed(): parts = lax.all_to_all(split_up(value, dim, peers), axis, 0, 0, tiled=True)  42.5 us
  transfers between devices with their start and end apart: 3, of which 3 were waited for; matrix products, arithmetic and copies ran while one was open for 3% of the time, Pallas kernels for 0%

profile of v1, /device:TPU:8, one launch (start us, length us, event | category | flops | bytes accessed | tf_op | source)
XLA Modules:
  0.0 551.9 jit_solution(13076691861495052865)
XLA Ops:
  7.2 0.7 rsqrt.15
  8.0 0.9 divide_convert_fusion
  8.9 1.7 pad_maximum_fusion.1
  10.6 0.9 copy.11
  11.5 0.1 compare_select_fusion
  11.6 10.8 %gather_fusion = s32[4096,6]{1,0:T(8,128)S(1)} fusion(s32[6,512]{0,1:T(8,128)S(1)} %copy.11, s32[4096]{0:T(1024)S(1)} %broadcast_clamp_fusion), kind=kCustom, calls=%fused_computation | custom fusion | bytes 212992 | tf_op jit(solution)/shard_map/jit(_take)/gather | solution.py:62
  22.5 3.8 compare_reduce_fusion
  27.0 0.2 convert_element_type.29
  27.1 61.7 %all-gather.2.cloned.1.call-done = bf16[4096,1024]{1,0:T(8,128)(2,1)} async-done(((bf16[128,1024]{1,0:T(8,128)(2,1)}), bf16[4096,1024]{1,0:T(8,128)(2,1)}) %all-gather.2.cloned.1.call-update) | async-done | bytes 8388624 | tf_op jit(solution)/shard_map/all_gather | solution.py:16
  88.8 17.6 %conditional.1 = (f32[16,48,256]{2,1,0:T(8,128)S(1)}, f32[16,48,1]{2,1,0:T(8,128)S(1)}) conditional(s32[]{:T(128)} %convert_element_type.26, () %tuple.20, (bf16[4096,1024]{1,0:T(8,128)(2,1)}, bf16[768,768]{1,0:T(8,128)(2,1)S(1)}, f32[768,768]{1,0:T(8,128)S(1)}, s32[6,4096]{0,1:T(8,128)}) %tuple.39), branch_computations={%region_1.2_spmd, %region_2.6_spmd} | conditional | flops 6475106304 | bytes 65716268 | solution.py:79
  88.8 2.9 copy.12
  91.7 1.1 convert_element_type.19
  92.7 0.2 multiply_reduce_fusion.1
  93.0 4.4 multiply_reduce_fusion
  97.4 6.9 %fusion = (f32[768]{0:T(1024)S(1)}, bf16[768,4096]{1,0:T(8,128)(2,1)S(1)}) fusion(f32[6,4096]{1,0:T(8,128)S(1)} %convert_element_type.19, f32[4096]{0:T(1024)S(1)} %multiply_reduce_fusion, f32[768]{0:T(1024)S(1)} %multiply_reduce_fusion.1, bf16[768,768]{1,0:T(8,128)(2,1)S(1)} %get-tuple-element.16, bf16[4096,1024]{1,0:T(8,128)(2,1)S(1)} %copy-done), kind=kOutput, calls=%fused_computation.3 | convolution fusion | flops 4853857280 | bytes 13917184 | tf_op jit(solution)/shard_map/cond/branch_1_fun/df,lf->dl/dot_general | solution.py:66
  104.2 1.8 fusion.4
  106.1 0.3 concatenate.17
  106.5 42.5 %all_to_all.5 = f32[16,48,257]{2,1,0:T(8,128)S(1)} all-to-all(f32[16,48,257]{2,1,0:T(8,128)S(1)} %pad_maximum_fusion), channel_id=1, replica_groups=mesh['blk'=32,'col'=16] {'col'}, dimensions={0} | all-to-all | bytes 1579008 | tf_op jit(solution)/shard_map/all_to_all | solution.py:27
  149.1 0.1 fusion.13
  149.2 0.2 multiply_reduce_fusion.2
  149.4 1.6 fusion.6
  151.0 223.0 %all-reduce.3.cloned.1.call-done = f32[1000,256]{1,0:T(8,128)} async-done(((f32[1000,256]{1,0:T(8,128)}), f32[1000,256]{1,0:T(8,128)}) %all-reduce.3.cloned.1.call-update) | async-done | bytes 1024016 | tf_op jit(solution)/shard_map/psum | solution.py:87
  374.1 169.1 %all-reduce.5.cloned.1.call-done = f32[1000,256]{1,0:T(8,128)} async-done(((f32[1000,256]{1,0:T(8,128)}), f32[1000,256]{1,0:T(8,128)}) %all-reduce.5.cloned.1.call-update) | async-done | bytes 1024016 | tf_op jit(solution)/shard_map/psum | solution.py:87
  543.2 2.2 copy.22
  (19 shorter events, 0.4 us)
Async XLA Ops:
  7.2 19.8 %copy-start.1 = (bf16[768,768]{1,0:T(8,128)(2,1)S(1)}, bf16[768,768]{1,0:T(8,128)(2,1)}, u32[]{:S(2)}) copy-start(bf16[768,768]{1,0:T(8,128)(2,1)} %param.9) | copy-start | bytes 3538948
  7.2 81.6 %all-gather.2.cloned.1.call-start = ((), (), s32[]{:S(2)}) async-start(), calls=%async_computation.1 | async-start | bytes 8650752 | tf_op jit(solution)/shard_map/all_gather | solution.py:16
  10.6 363.5 %all-reduce.3.cloned.1.call-start = ((), (), s32[]{:S(2)}) async-start(), calls=%async_computation.2 | async-start | bytes 2048000 | tf_op jit(solution)/shard_map/psum | solution.py:87
  88.8 60.6 %copy-start.3 = (s32[48]{0:T(128)S(1)}, s32[48]{0:T(128)}, u32[]{:S(2)}) copy-start(s32[48]{0:T(128)} %param.15) | copy-start | bytes 580
  91.7 5.7 %copy-start = (bf16[4096,1024]{1,0:T(8,128)(2,1)S(1)}, bf16[4096,1024]{1,0:T(8,128)(2,1)}, u32[]{:S(2)}) copy-start(bf16[4096,1024]{1,0:T(8,128)(2,1)} %get-tuple-element.17) | copy-start | bytes 25165828 | tf_op jit(solution)/shard_map/cond
  149.4 396.1 %copy-start.2 = (f32[48,256]{1,0:T(8,128)}, f32[48,256]{1,0:T(8,128)S(1)}, u32[]{:S(2)}) copy-start(f32[48,256]{1,0:T(8,128)S(1)} %get-tuple-element.45) | copy-start | bytes 147460
  151.0 392.2 %all-reduce.5.cloned.1.call-start = ((), (), s32[]{:S(2)}) async-start(), calls=%async_computation.3 | async-start | bytes 2048000 | tf_op jit(solution)/shard_map/psum | solution.py:87
Sparse Core Ops, SparseCore 0:
  10.7 78.0 all-gather.1
  151.1 222.9 all-reduce.2
  377.0 166.0 all-reduce.4
